TPU v7x, 512 devices: a whole 4x8x8 slice. The times are simulated.
512 devices in a mesh: gx: 4 (over x), gy: 8 (over z), gz: 16 (over y, core).
Axes of the slice: x: 4, y: 8, z: 8, core: 2. Of those that a mesh axis runs over, the one named last changes fastest.
Arguments:
- positions: float32 [3, 262144], P(None, ('gx', 'gy', 'gz')), may hold values from -6 to 6
- frames: float32 [128, 3, 4096], P(None, None, ('gy', 'gz')), may hold values from -6 to 6
- path_slot: int32 [512, 32], P(('gx', 'gy', 'gz')), may hold values from 0 to 511, as said below
- path_count: int32 [512], replicated, may hold values from 1 to 32, 4096 in all
- path_order: int32 [4096], replicated, may hold values from 0 to 4095, each once
- frame_rank: int32 [128], replicated, may hold values from 0 to 127, each once
Outputs:
- forces: float32 [3, 262144], P(None, ('gx', 'gy', 'gz'))
- path_cv: float32 [2], replicated
Inputs may be any that keep to these rules, and one draw needn't show every extreme that they name: `path_slot`: within one domain's row the 32 local atom indices are all different.
All inputs are finite; a program needn't handle non-finite values.
Results may differ from a plain program's by a relative error of at most 0.00013.
Values sent between devices are 32-bit elements; how exact they have to be, the bound alone decides.
No kernel may reach another device: no remote copies, remote signals or barrier semaphores. Data moves between devices by JAX's collectives and lax.ppermute only.
A program may use at most 64 MiB of HBM per device.

v0:
```python
import jax
import jax.numpy as jnp
from jax import lax
from jax.sharding import Mesh
from jax.sharding import PartitionSpec as P

P_SIZE = 4096
GX_GY_GZ = ("gx", "gy", "gz_0", "gz_1")
GY_GZ = ("gy", "gz_0", "gz_1")
STRENGTH = 20.0
S_HOME = 0.5
KAPPA_S = 0.5
KAPPA_Z = 0.05
PAIR_SCALE = 0.02
WIDTH_SQ = 4.0


def one_axis_at_a_time(array, axes):
    for axis in axes:
        array = lax.psum(array, axis)
    return array


def pair_block(block_pos, all_pos):
    diff = block_pos[:, :, None] - all_pos[:, None, :]
    dist_sq = jnp.sum(diff * diff, axis=0)
    weight = PAIR_SCALE * jnp.exp(-dist_sq / WIDTH_SQ)
    return jnp.sum(weight[None] * diff, axis=2)


def domain_forces(local):
    atoms = local.shape[1]
    rows = 256
    blocks = local.reshape(3, atoms // rows, rows).transpose(1, 0, 2)
    result = lax.map(lambda block: pair_block(block, local), blocks)
    return result.transpose(1, 0, 2).reshape(3, atoms)


def slot_ids(path_count, path_order, slots):
    offsets = jnp.cumsum(path_count) - path_count
    steps_k = jnp.arange(slots, dtype=jnp.int32)
    live = steps_k[None, :] < path_count[:, None]
    place = jnp.clip(offsets[:, None] + steps_k[None, :], 0, P_SIZE - 1)
    ids = jnp.where(live, path_order[place], -1)
    return (ids, live)


def cv_terms(dist, frame_rank):
    frames_n = dist.shape[0]
    expo = -STRENGTH * dist
    top = jnp.max(expo)
    expd = jnp.exp(expo - top)
    total = jnp.sum(expd)
    weight = expd / total
    progress_rank = frame_rank.astype(jnp.float32) / (frames_n - 1.0)
    s_value = jnp.sum(progress_rank * weight)
    z_value = -(top + jnp.log(total)) / STRENGTH
    grads = (
        KAPPA_S * P_SIZE * (s_value - S_HOME) * -STRENGTH * weight * (progress_rank - s_value)
        + KAPPA_Z * P_SIZE * z_value * weight
    )
    return (s_value, z_value, grads)


def summed_terms(partial_value, frame_rank):
    dist = one_axis_at_a_time(partial_value, GX_GY_GZ)
    return cv_terms(dist, frame_rank)


def body(positions, frames, path_slot, path_count, path_order, frame_rank):
    slots = path_slot.shape[1]
    local_slot = path_slot[0]
    ids, live = slot_ids(path_count, path_order, slots)
    path_pos = jnp.take(positions, local_slot, axis=1)
    here = lax.axis_index(GX_GY_GZ)
    my_ids = lax.dynamic_slice_in_dim(ids, here, 1, 0)[0]
    mask = lax.dynamic_slice_in_dim(live, here, 1, 0)[0].astype(jnp.float32)
    whole = lax.all_gather(frames, GY_GZ, axis=2, tiled=True)
    refs = jnp.take(whole, jnp.clip(my_ids, 0, P_SIZE - 1), axis=2)
    delta = path_pos[None] - refs
    partial_value = jnp.sum(jnp.sum(delta * delta, axis=1) * mask[None], axis=1) / P_SIZE
    s_value, z_value, grads = summed_terms(partial_value, frame_rank)
    bias = (
        -(2.0 / P_SIZE)
        * jnp.einsum("f,fcm->cm", grads, delta, precision=lax.Precision.HIGHEST)
        * mask[None]
    )
    forces = domain_forces(positions)
    forces = forces.at[:, local_slot].add(bias)
    return (forces, jnp.stack([s_value, z_value]))


def solution(mesh):
    finer = Mesh(
        mesh.devices.reshape(mesh.shape["gx"], mesh.shape["gy"], 8, 2), ("gx", "gy", "gz_0", "gz_1")
    )
    return jax.shard_map(
        body,
        mesh=finer,
        in_specs=(P(None, GX_GY_GZ), P(None, None, GY_GZ), P(GX_GY_GZ, None), P(), P(), P()),
        out_specs=(P(None, GX_GY_GZ), P()),
        check_vma=False,
    )
```

profile of v0, /device:TPU:1, one launch (start us, length us, event | category | flops | bytes accessed | tf_op | source)
XLA Modules:
  0.0 190.1 jit_solution(15374449258505947878)
XLA Ops:
  7.2 0.0 copy-start
  7.2 0.0 all-gather.2.cloned.1.call-start
  7.2 0.7 all-gather.2.cloned.1.call-update
  7.9 1.0 reduce-window.9
  8.9 0.1 slice.7
  9.0 0.1 slice_reduce_fusion
  9.1 0.8 bitcast_subtract_fusion.1
  9.9 0.1 compare_select_fusion
  10.0 0.1 reshape.176
  10.2 0.0 copy-done
  10.2 0.0 copy-start.1
  10.2 90.5 %gather_fusion.1 = s32[16384]{0:T(1024)S(1)} fusion(s32[4096]{0:T(1024)S(1)} %copy-done, s32[16384]{0:T(1024)S(1)} %broadcast_clamp_fusion), kind=kCustom, calls=%fused_computation.1 | custom fusion | bytes 196608 | tf_op jit(solution)/shard_map/gather | solution.py:44
  100.8 0.1 reshape.175
  100.9 0.0 copy-done.1
  100.9 0.1 copy.21
  101.0 0.0 copy-start.4
  101.0 0.0 copy-start.2
  101.1 1.5 while.10
  101.1 0.2 fusion.25
  101.3 0.1 exponential_multiply_fusion.2
  101.4 0.4 fusion.26
  101.8 0.2 fusion.25
  102.0 0.1 exponential_multiply_fusion.2
  102.1 0.4 fusion.26
  102.5 0.1 copy.20
  102.7 0.0 copy-done.4
  102.7 0.6 gather_fusion
  103.3 0.0 copy-done.2
  103.3 0.1 iota_compare_fusion
  103.5 0.1 select_bitcast_fusion
  103.6 0.0 copy-start.3
  103.6 0.0 all-gather.2.cloned.1.call-done
  103.6 10.7 %copy.22 = f32[128,3,4096]{0,1,2:T(4,128)} copy(f32[128,3,4096]{0,2,1:T(8,128)} %all-gather.2.cloned.1.call-done) | data formatting | bytes 12582912 | tf_op jit(solution)/shard_map/all_gather | solution.py:78
  114.3 4.0 %gather_fusion.2 = f32[32,128,3]{1,2,0:T(4,128)S(1)} fusion(f32[128,3,4096]{0,1,2:T(4,128)} %copy.22, s32[1024]{0:T(1024)S(1)} %pad_clamp_fusion), kind=kCustom, calls=%fused_computation.2 | custom fusion | bytes 98432 | tf_op jit(solution)/shard_map/jit(_take)/gather | solution.py:79
  118.3 0.1 multiply_reduce_fusion
  118.4 0.1 multiply_reduce_fusion.1
  118.5 9.3 %psum.28 = f32[128]{0:T(128)S(1)} all-reduce(f32[128]{0:T(128)S(1)} %broadcast_multiply_fusion), channel_id=1, replica_groups=mesh['gx'=4,'gy'=8,'gz_0'=8,'gz_1'=2] {'gx'}, use_global_device_ids=true, to_apply=%region_8.9 | all-reduce | flops 128 | bytes 1024 | tf_op jit(solution)/shard_map/psum | solution.py:20
  127.8 19.5 %psum.29 = f32[128]{0:T(128)S(1)} all-reduce(f32[128]{0:T(128)S(1)} %psum.28), channel_id=1, replica_groups=mesh['gx'=4,'gy'=8,'gz_0'=8,'gz_1'=2] {'gy'}, use_global_device_ids=true, to_apply=%region_9.10 | all-reduce | flops 128 | bytes 1024 | tf_op jit(solution)/shard_map/psum | solution.py:20
  147.3 13.8 %psum.30 = f32[128]{0:T(128)S(1)} all-reduce(f32[128]{0:T(128)S(1)} %psum.29), channel_id=1, replica_groups=mesh['gx'=4,'gy'=8,'gz_0'=8,'gz_1'=2] {'gz_0'}, use_global_device_ids=true, to_apply=%region_10.11 | all-reduce | flops 128 | bytes 1024 | tf_op jit(solution)/shard_map/psum | solution.py:20
  161.1 12.3 %psum.31 = f32[128]{0:T(128)S(1)} all-reduce(f32[128]{0:T(128)S(1)} %psum.30), channel_id=1, replica_groups=mesh['gx'=4,'gy'=8,'gz_0'=8,'gz_1'=2] {'gz_1'}, use_global_device_ids=true, to_apply=%region_11.12 | all-reduce | flops 128 | bytes 1024 | tf_op jit(solution)/shard_map/psum | solution.py:20
  173.4 0.6 multiply_reduce_fusion.3
  174.0 1.3 fusion.21
  176.6 0.0 copy-done.3
  176.6 2.0 %multiply_reduce_fusion.2 = (f32[]{:T(128)}, f32[128]{0:T(128)S(1)}) fusion(s32[128]{0:T(128)S(1)} %copy-done.3, f32[]{:T(128)} %fusion.21, f32[]{:T(128)} %multiply_reduce_fusion.3, f32[128]{0:T(128)S(1)} %psum.31), kind=kLoop, calls=%fused_computation.47 | loop fusion | flops 895 | bytes 1548 | tf_op jit(solution)/shard_map/reduce_sum | solution.py:56
  179.3 0.9 fusion.2
  180.2 0.1 copy.25
  180.3 1.0 scatter_custom_fusion
  181.3 0.7 copy.23
  182.0 1.3 pad_maximum_fusion
  (15 shorter events, 0.2 us)
Async XLA Ops:
  7.2 3.0 %copy-start = (s32[4096]{0:T(1024)S(1)}, s32[4096]{0:T(1024)}, u32[]{:S(2)}) copy-start(s32[4096]{0:T(1024)} %param.12) | copy-start | bytes 49156
  7.2 96.4 %all-gather.2.cloned.1.call-start = ((), (), s32[]{:S(2)}) async-start(), calls=%async_computation | async-start | bytes 6340608 | tf_op jit(solution)/shard_map/all_gather | solution.py:78
  10.2 90.7 %copy-start.1 = (f32[3,512]{1,0:T(4,128)S(1)}, f32[3,512]{1,0:T(4,128)}, u32[]{:S(2)}) copy-start(f32[3,512]{1,0:T(4,128)} %param.8) | copy-start | bytes 18436
  101.0 1.6 copy-start.4
  101.0 2.2 %copy-start.2 = (s32[512]{0:T(512)S(1)}, s32[512]{0:T(512)}, u32[]{:S(2)}) copy-start(s32[512]{0:T(512)} %param.11) | copy-start | bytes 6148
  103.6 73.0 %copy-start.3 = (s32[128]{0:T(128)S(1)}, s32[128]{0:T(128)}, u32[]{:S(2)}) copy-start(s32[128]{0:T(128)} %param.13) | copy-start | bytes 1540
Sparse Core Ops, SparseCore 0:
  11.2 91.8 all-gather.1
where the time goes:
time: 191 us; the launch traced here: 190 us
  local copies, waits for them, and re-layouts  107 us (56%)
  blocking collectives  54.9 us (29%)
  between operations  16.3 us (9%)
  other arithmetic  9.86 us (5%)
    gather x2, local copies, waits for them, and re-layouts, slot_ids(): ids = jnp.where(live, path_order[place], -1)  90.7 us
    psum x4, blocking collectives, one_axis_at_a_time(): array = lax.psum(array, axis)  54.9 us
    all_gather x1, local copies, waits for them, and re-layouts, body(): whole = lax.all_gather(frames, GY_GZ, axis=2, tiled=True)  10.7 us
    gather x1, local copies, waits for them, and re-layouts, body(): refs = jnp.take(whole, jnp.clip(my_ids, 0, P_SIZE - 1), axis=2)  3.99 us
  transfers between devices with their start and end apart: 1, of which 0 were waited for; matrix products, arithmetic and copies ran while one was open for 50% of the time, Pallas kernels for 0%

commit v1 on v0

--- a/solution.py
+++ b/solution.py
@@ -75,7 +75,9 @@
     here = lax.axis_index(GX_GY_GZ)
     my_ids = lax.dynamic_slice_in_dim(ids, here, 1, 0)[0]
     mask = lax.dynamic_slice_in_dim(live, here, 1, 0)[0].astype(jnp.float32)
-    whole = lax.all_gather(frames, GY_GZ, axis=2, tiled=True)
+    whole = jnp.concatenate(
+        lax.all_to_all(jnp.stack([frames] * lax.axis_size(GY_GZ)), GY_GZ, 0, 0), axis=2
+    )
     refs = jnp.take(whole, jnp.clip(my_ids, 0, P_SIZE - 1), axis=2)
     delta = path_pos[None] - refs
     partial_value = jnp.sum(jnp.sum(delta * delta, axis=1) * mask[None], axis=1) / P_SIZE

time: 191 us -> 280 us (1.47)
  waiting for transfers between devices: 0.68 us -> 67.5 us
  starting transfers between devices: 0.04 us -> 18.9 us
  local copies, waits for them, and re-layouts: 107 us -> 123 us
  between operations: 16.3 us -> 2.92 us
    all_to_all x0 -> x1, waiting for transfers between devices: none -> 67.5 us  [body(): lax.all_to_all(jnp.stack([frames] * lax.axis_size(GY_GZ)), GY_GZ, 0, 0)]
    all_to_all x0 -> x1, starting transfers between devices: none -> 18.9 us  [body(): lax.all_to_all(jnp.stack([frames] * lax.axis_size(GY_GZ)), GY_GZ, 0, 0)]
    reshape x0 -> x1, local copies, waits for them, and re-layouts: none -> 18.7 us  [body(): jnp.concatenate(lax.all_to_all(jnp.stack([frames] * lax.axis_size(GY_GZ))...]
    all_gather x1 -> x0, local copies, waits for them, and re-layouts: 10.7 us -> none  [body(): whole = lax.all_gather(frames, GY_GZ, axis=2, tiled=True)]
    another operation x1 -> x2, local copies, waits for them, and re-layouts: 0.12 us -> 4.38 us  [the longest x1 4.26 us: body(): jnp.stack([frames] * lax.axis_size(GY_GZ))]
    all_to_all x0 -> x1, local copies, waits for them, and re-layouts: none -> 3.49 us  [body(): lax.all_to_all(jnp.stack([frames] * lax.axis_size(GY_GZ)), GY_GZ, 0, 0)]
  transfers between devices with their start and end apart: 1 -> 1, of which waited for: 0 -> 1; matrix products, arithmetic and copies ran while one was open for 50% -> 34% of each run, Pallas kernels for 0% -> 0%
where the time goes in v1:
time: 280 us; the launch traced here: 279 us
  local copies, waits for them, and re-layouts  123 us (44%)
  waiting for transfers between devices  67.5 us (24%)
  blocking collectives  57.5 us (21%)
  starting transfers between devices  18.9 us (7%)
  other arithmetic  8.5 us (3%)
  between operations  2.92 us (1%)
    gather x2, local copies, waits for them, and re-layouts, slot_ids(): ids = jnp.where(live, path_order[place], -1)  90.7 us
    all_to_all x1, waiting for transfers between devices, body(): lax.all_to_all(jnp.stack([frames] * lax.axis_size(GY_GZ)), GY_GZ, 0, 0)  67.5 us
    psum x4, blocking collectives, one_axis_at_a_time(): array = lax.psum(array, axis)  57.5 us
    all_to_all x1, starting transfers between devices, body(): lax.all_to_all(jnp.stack([frames] * lax.axis_size(GY_GZ)), GY_GZ, 0, 0)  18.9 us
    reshape x1, local copies, waits for them, and re-layouts, body(): jnp.concatenate(lax.all_to_all(jnp.stack([frames] * lax.axis_size(GY_GZ))...  18.7 us
  transfers between devices with their start and end apart: 1, of which 1 were waited for; matrix products, arithmetic and copies ran while one was open for 34% of the time, Pallas kernels for 0%

profile of v1, /device:TPU:1, one launch (start us, length us, event | category | flops | bytes accessed | tf_op | source)
XLA Modules:
  0.0 279.4 jit_solution(13632184589611578478)
XLA Ops:
  0.6 0.0 copy-start
  0.6 4.3 %stack.8 = f32[128,128,3,32]{1,3,2,0:T(8,128)} broadcast(f32[128,3,32]{0,2,1:T(8,128)} %param.9), dimensions={1,2,3} | broadcast | bytes 6340608 | tf_op jit(solution)/shard_map/stack | solution.py:79
  4.9 0.0 copy-start.2
  4.9 18.9 %all-to-all-start = ((f32[128,128,3,32]{1,3,2,0:T(8,128)}), f32[128,128,3,32]{1,3,2,0:T(8,128)}, u32[]{:S(2)}, u32[]{:S(2)}) async-start(f32[128,128,3,32]{1,3,2,0:T(8,128)} %stack.8), calls=%async_computation | async-start | bytes 12582912 | tf_op jit(solution)/shard_map/all_to_all | solution.py:79
  23.9 0.0 copy-done.2
  23.9 0.3 reduce-window.9
  24.2 0.1 slice.7
  24.3 0.1 slice_reduce_fusion
  24.4 0.1 bitcast_subtract_fusion.1
  24.5 0.1 compare_select_fusion
  24.6 0.1 reshape.186
  24.8 0.0 copy-done
  24.8 0.0 copy-start.1
  24.8 90.5 %gather_fusion.1 = s32[16384]{0:T(1024)S(1)} fusion(s32[4096]{0:T(1024)S(1)} %copy-done, s32[16384]{0:T(1024)S(1)} %broadcast_clamp_fusion), kind=kCustom, calls=%fused_computation.1 | custom fusion | bytes 196608 | tf_op jit(solution)/shard_map/gather | solution.py:44
  115.4 0.1 reshape.185
  115.5 0.0 copy-done.1
  115.5 0.1 copy.23
  115.6 0.0 copy-start.4
  115.7 1.4 while.10
  115.7 0.2 fusion.25
  115.9 0.1 exponential_multiply_fusion.2
  116.0 0.4 fusion.26
  116.4 0.2 fusion.25
  116.6 0.1 exponential_multiply_fusion.2
  116.7 0.4 fusion.26
  117.1 0.1 copy.22
  117.3 0.0 copy-done.4
  117.3 0.6 gather_fusion
  117.9 0.1 iota_compare_fusion
  118.1 0.1 select_bitcast_fusion
  118.2 67.5 %all-to-all-done = f32[128,128,3,32]{1,3,2,0:T(8,128)} async-done(((f32[128,128,3,32]{1,3,2,0:T(8,128)}), f32[128,128,3,32]{1,3,2,0:T(8,128)}, u32[]{:S(2)}, u32[]{:S(2)}) %all-to-all-start) | async-done | bytes 6291488 | tf_op jit(solution)/shard_map/all_to_all | solution.py:79
  185.6 3.5 %copy.24 = f32[128,128,3,32]{1,3,0,2:T(8,128)S(1)} copy(f32[128,128,3,32]{1,3,2,0:T(8,128)} %all-to-all-done) | data formatting | bytes 12582912 | tf_op jit(solution)/shard_map/all_to_all | solution.py:79
  189.1 0.0 copy-start.3
  189.1 18.7 %copy.25 = f32[128,3,4096]{0,1,2:T(4,128)} copy(f32[128,3,4096]{0,2,1:T(8,128)S(1)} %bitcast.55) | data formatting | bytes 12582912 | tf_op jit(solution)/shard_map/reshape | solution.py:78
  207.8 4.0 %gather_fusion.2 = f32[32,128,3]{1,2,0:T(4,128)S(1)} fusion(f32[128,3,4096]{0,1,2:T(4,128)} %copy.25, s32[1024]{0:T(1024)S(1)} %pad_clamp_fusion), kind=kCustom, calls=%fused_computation.2 | custom fusion | bytes 98432 | tf_op jit(solution)/shard_map/jit(_take)/gather | solution.py:81
  211.8 0.1 multiply_reduce_fusion
  212.0 0.1 multiply_reduce_fusion.1
  212.0 8.5 %psum.28 = f32[128]{0:T(128)S(1)} all-reduce(f32[128]{0:T(128)S(1)} %broadcast_multiply_fusion), channel_id=1, replica_groups=mesh['gx'=4,'gy'=8,'gz_0'=8,'gz_1'=2] {'gx'}, use_global_device_ids=true, to_apply=%region_8.9 | all-reduce | flops 128 | bytes 1024 | tf_op jit(solution)/shard_map/psum | solution.py:20
  220.5 16.3 %psum.29 = f32[128]{0:T(128)S(1)} all-reduce(f32[128]{0:T(128)S(1)} %psum.28), channel_id=1, replica_groups=mesh['gx'=4,'gy'=8,'gz_0'=8,'gz_1'=2] {'gy'}, use_global_device_ids=true, to_apply=%region_9.10 | all-reduce | flops 128 | bytes 1024 | tf_op jit(solution)/shard_map/psum | solution.py:20
  236.8 20.3 %psum.30 = f32[128]{0:T(128)S(1)} all-reduce(f32[128]{0:T(128)S(1)} %psum.29), channel_id=1, replica_groups=mesh['gx'=4,'gy'=8,'gz_0'=8,'gz_1'=2] {'gz_0'}, use_global_device_ids=true, to_apply=%region_10.11 | all-reduce | flops 128 | bytes 1024 | tf_op jit(solution)/shard_map/psum | solution.py:20
  257.1 12.5 %psum.31 = f32[128]{0:T(128)S(1)} all-reduce(f32[128]{0:T(128)S(1)} %psum.30), channel_id=1, replica_groups=mesh['gx'=4,'gy'=8,'gz_0'=8,'gz_1'=2] {'gz_1'}, use_global_device_ids=true, to_apply=%region_11.12 | all-reduce | flops 128 | bytes 1024 | tf_op jit(solution)/shard_map/psum | solution.py:20
  269.6 0.6 multiply_reduce_fusion.3
  270.2 1.3 fusion.21
  272.8 0.0 copy-done.3
  272.8 2.0 multiply_reduce_fusion.2
  275.5 0.9 fusion.2
  276.4 0.1 copy.28
  276.5 1.0 scatter_custom_fusion
  277.5 0.7 copy.26
  278.2 1.3 pad_maximum_fusion
  (15 shorter events, 0.2 us)
Async XLA Ops:
  0.6 24.2 %copy-start = (s32[4096]{0:T(1024)S(1)}, s32[4096]{0:T(1024)}, u32[]{:S(2)}) copy-start(s32[4096]{0:T(1024)} %param.12) | copy-start | bytes 49156
  4.9 19.0 %copy-start.2 = (s32[512]{0:T(512)S(1)}, s32[512]{0:T(512)}, u32[]{:S(2)}) copy-start(s32[512]{0:T(512)} %param.11) | copy-start | bytes 6148
  4.9 180.7 %all-to-all-start = ((f32[128,128,3,32]{1,3,2,0:T(8,128)}), f32[128,128,3,32]{1,3,2,0:T(8,128)}, u32[]{:S(2)}, u32[]{:S(2)}) async-start(f32[128,128,3,32]{1,3,2,0:T(8,128)} %stack.8), calls=%async_computation | async-start | bytes 12582912 | tf_op jit(solution)/shard_map/all_to_all | solution.py:79
  24.8 90.7 %copy-start.1 = (f32[3,512]{1,0:T(4,128)S(1)}, f32[3,512]{1,0:T(4,128)}, u32[]{:S(2)}) copy-start(f32[3,512]{1,0:T(4,128)} %param.8) | copy-start | bytes 18436
  115.6 1.6 copy-start.4
  189.1 83.6 %copy-start.3 = (s32[128]{0:T(128)S(1)}, s32[128]{0:T(128)}, u32[]{:S(2)}) copy-start(s32[128]{0:T(128)} %param.13) | copy-start | bytes 1540
